TPU v7x, 32 devices: a whole 2x2x4 slice. The times are simulated.
32 devices in a mesh: groups: 2 (over x), samp: 16 (over z, y, core).
Axes of the slice: x: 2, y: 2, z: 4, core: 2. Of those that a mesh axis runs over, the one named last changes fastest.
Arguments:
- dosage: bfloat16 [8192, 8192], P(('groups', 'samp')), parts along dimension 0, may hold values from 0 to 2
- covariates: bfloat16 [8192, 96], P(('groups', 'samp')), parts along dimension 0, may hold values from -8 to 8
- expression: bfloat16 [8192, 8192], P('groups', 'samp'), parts along dimension 0, may hold values from -10 to 10
- block_index: int32 [4, 1024], P('groups'), parts along dimension 0, may hold values from 0 to 8191
- expr_row: int32 [8192], P('groups'), parts along dimension 0, may hold values from 0 to 4095, each once
Outputs:
- zscore: float32 [4096, 8192], P('groups', 'samp'), parts along dimension 0
There are 2 independent parts, one for each index of `groups`. A program takes and returns all parts, laid end to end along the dimension named above; each array names one. Nothing has to cross between parts.
Inputs may be any that keep to these rules, and one draw needn't show every extreme that they name: `expr_row`: every expression row appears once.
All inputs are finite; a program needn't handle non-finite values.
Results may differ from a plain program's by a relative error of at most 0.0029.
Values may be sent and summed in bfloat16 or wider, within the bound.
A program may use at most 192 MiB of HBM per device.

v0:
```python
import math

import jax
import jax.numpy as jnp
from jax import lax
from jax.sharding import PartitionSpec as P

epsilon = 1e-06


def as_sent(x):

    def short(part):
        return part.astype(jnp.bfloat16) if part.dtype == jnp.float32 else part

    return jax.tree.map(short, x)


def adjust(picked, covariates, factor, loads):
    coeffs = jax.scipy.linalg.cho_solve((factor, True), loads)
    fitted = jnp.dot(covariates.astype(jnp.float32), coeffs, precision=lax.Precision.HIGHEST)
    return (picked.astype(jnp.float32) - fitted).astype(jnp.bfloat16)


def make_fold(expression, expr_row):

    def fold(carry, pieces, start):
        sums, norms = carry
        rows = jnp.take(expression, expr_row, axis=0)
        sums = tuple(
            (
                jnp.einsum("sv,sg->vg", piece, rows, preferred_element_type=jnp.float32)
                for piece in pieces
            )
        )
        return (sums, norms)

    return fold


def finish(products, resid, panel_norm, scale):
    resid_norm = lax.psum(jnp.sum(jnp.square(resid.astype(jnp.float32)), axis=0), "samp")
    return (
        scale
        * products
        * lax.rsqrt(resid_norm + epsilon)[:, None]
        * lax.rsqrt(panel_norm + epsilon)[None, :]
    )


def local(dosage, covariates, expression, block_index, expr_row):
    blocks = block_index.shape[0]
    width = block_index.shape[1]
    covars = covariates.shape[1]
    genes_here = expression.shape[1]
    scale = math.sqrt(expr_row.shape[0] - covars - 1)
    fold = make_fold(expression, expr_row)
    panel_norm = jnp.sum(jnp.square(expression.astype(jnp.float32)), axis=0)
    local_gram = jnp.dot(covariates.T, covariates, preferred_element_type=jnp.float32)
    picks = [jnp.take(dosage, block_index[block], axis=1) for block in range(blocks)]
    partials = [
        jnp.dot(covariates.T, picked, preferred_element_type=jnp.float32) for picked in picks
    ]
    empty_sum = jnp.zeros((width, genes_here), jnp.float32)
    results = []
    gram, loads = lax.psum((local_gram, jnp.stack(partials)), "samp")
    factor = jnp.linalg.cholesky(gram)
    resids = tuple(
        (adjust(picks[block], covariates, factor, loads[block]) for block in range(blocks))
    )
    start_norms = ()
    start_sums = tuple((empty_sum for block in range(blocks)))
    sums, norms = fold(
        (start_sums, start_norms),
        jax.tree.map(
            lambda part: lax.all_gather(part, "samp", axis=0, tiled=True), as_sent(resids)
        ),
        jnp.int32(0),
    )
    for block in range(blocks):
        results.append(finish(sums[block], resids[block], panel_norm, scale))
    return jnp.concatenate(results, axis=0)


def solution(mesh):
    placed = (
        P(("groups", "samp"), None),
        P(("groups", "samp"), None),
        P("groups", "samp"),
        P("groups", None),
        P("groups"),
    )
    return jax.shard_map(
        local, mesh=mesh, in_specs=placed, out_specs=P("groups", "samp"), check_vma=False
    )
```

profile of v0, /device:TPU:9, one launch (start us, length us, event | category | flops | bytes accessed | tf_op | source)
XLA Modules:
  0.0 293.8 jit_solution(14813910648524335252)
XLA Ops:
  6.5 0.8 fusion.27
  7.4 6.4 %copy.6 = bf16[256,8192]{0,1:T(8,128)(2,1)} copy(bf16[256,8192]{1,0:T(8,128)(2,1)} %param.9) | data formatting | bytes 8388608 | tf_op args[0]
  13.7 6.2 %gather_fusion.2 = bf16[1024,256]{1,0:T(8,128)(2,1)S(1)} fusion(bf16[256,8192]{0,1:T(8,128)(2,1)} %copy.6, s32[1024]{0:T(1024)S(1)} %fusion.22), kind=kCustom, calls=%fused_computation.1.clone | custom fusion | bytes 1052672 | tf_op jit(solution)/shard_map/jit(_take)/gather | solution.py:60
  19.9 6.2 %gather_fusion.1 = bf16[1024,256]{1,0:T(8,128)(2,1)S(1)} fusion(bf16[256,8192]{0,1:T(8,128)(2,1)} %copy.6, s32[1024]{0:T(1024)S(1)} %fusion.21), kind=kCustom, calls=%fused_computation.clone | custom fusion | bytes 1052672 | tf_op jit(solution)/shard_map/jit(_take)/gather | solution.py:60
  26.1 0.2 copy.7
  26.4 0.2 copy.11
  26.6 0.2 convolution_bitcast_fusion.2
  26.8 0.2 convolution_bitcast_fusion.3
  27.0 0.9 pad_maximum_fusion.1
  28.1 0.1 fusion.28
  28.2 49.5 %psum.28 = f32[96,96]{0,1:T(8,128)S(1)} all-reduce(f32[96,96]{0,1:T(8,128)S(1)} %fusion.28), channel_id=1, replica_groups=mesh['groups'=2,'samp'=16] {'samp'}, use_global_device_ids=true, to_apply=%region_0.2 | all-reduce | flops 9216 | bytes 73728 | tf_op jit(solution)/shard_map/psum | solution.py:66
  77.7 0.1 copy.9
  77.8 8.8 %cholesky.18 = f32[96,96]{1,0:T(8,128)S(1)} custom-call(f32[96,96]{1,0:T(8,128)S(1)} %fusion.19), custom_call_target="Cholesky" | custom-call | tf_op jit(solution)/shard_map/jit(cholesky)/cholesky | solution.py:67
  86.6 0.7 compare_reduce_fusion
  87.4 0.7 fusion.12
  88.1 7.4 %custom-call.9 = f32[1,96,96]{1,2,0:T(8,128)S(1)} custom-call(f32[1,96,96]{2,1,0:T(8,128)S(1)} %fusion.12), custom_call_target="InvertDiagBlocksLowerTriangular" | custom-call | tf_op jit(solution)/shard_map/jit(_cho_solve)/triangular_solve | solution.py:20
  95.4 25.0 %all-reduce.3.cloned.1.call-done = f32[2,96,1024]{2,1,0:T(8,128)} async-done(((f32[2,96,1024]{2,1,0:T(8,128)}), f32[2,96,1024]{2,1,0:T(8,128)}) %all-reduce.3.cloned.1.call-update) | async-done | bytes 786448 | tf_op jit(solution)/shard_map/psum | solution.py:66
  120.4 1.5 fusion.9
  121.9 0.5 fusion.16
  122.4 1.5 multiply_reduce_fusion.2
  123.9 0.0 all-gather.5.cloned.1.call-start
  124.0 1.5 fusion.8
  125.5 0.5 fusion.13
  125.9 1.5 multiply_reduce_fusion.1
  127.5 20.2 %gather_fusion = bf16[4096,512]{1,0:T(8,128)(2,1)} fusion(bf16[4096,512]{1,0:T(8,128)(2,1)} %param.11, s32[4096]{0:T(1024)S(1)} %fusion.20), kind=kCustom, calls=%fused_computation.2 | custom fusion | bytes 8404992 | tf_op jit(solution)/shard_map/jit(_take)/gather | solution.py:29
  147.7 3.1 %multiply_reduce_fusion = f32[512]{0:T(512)S(1)} fusion(bf16[4096,512]{1,0:T(8,128)(2,1)} %param.11), kind=kLoop, calls=%fused_computation.3 | loop fusion | flops 6290944 | bytes 4196352 | tf_op jit(solution)/shard_map/reduce_sum | solution.py:58
  150.8 28.5 %all-reduce = (f32[1024]{0:T(1024)S(1)}, f32[1024]{0:T(1024)S(1)}) all-reduce(f32[1024]{0:T(1024)S(1)} %get-tuple-element.11, f32[1024]{0:T(1024)S(1)} %get-tuple-element.13), channel_id=1, replica_groups=mesh['groups'=2,'samp'=16] {'samp'}, use_global_device_ids=true, to_apply=%region_8.11 | all-reduce | flops 2048 | bytes 16384 | tf_op jit(solution)/shard_map/psum | solution.py:42
  179.3 21.3 %all-gather.3.cloned.1.call-done = bf16[4096,1024]{1,0:T(8,128)(2,1)} async-done(((bf16[256,1024]{1,0:T(8,128)(2,1)}), bf16[4096,1024]{1,0:T(8,128)(2,1)}) %all-gather.3.cloned.1.call-update) | async-done | bytes 8388624 | tf_op jit(solution)/shard_map/all_gather | solution.py:76
  200.6 9.1 %multiply_multiply_fusion.1 = f32[1024,512]{1,0:T(8,128)S(1)} fusion(bf16[4096,1024]{1,0:T(8,128)(2,1)} %all-gather.3.cloned.1.call-done, bf16[4096,512]{1,0:T(8,128)(2,1)} %gather_fusion, pred[4096]{0:T(1024)(128)(4,1)S(1)} %compare_and_fusion, f32[512]{0:T(512)S(1)} %add_rsqrt_fusion, f32[1024]{0:T(1024)S(1)} %get-tuple-element.16), kind=kOutput, calls=%fused_computation.7 | convolution fusion | flops 4298113024 | bytes 14690304 | tf_op jit(solution)/shard_map/sv,sg->vg/dot_general | solution.py:32
  209.8 65.9 %all-gather.5.cloned.1.call-done = bf16[4096,1024]{1,0:T(8,128)(2,1)} async-done(((bf16[256,1024]{1,0:T(8,128)(2,1)}), bf16[4096,1024]{1,0:T(8,128)(2,1)}) %all-gather.5.cloned.1.call-update) | async-done | bytes 8388624 | tf_op jit(solution)/shard_map/all_gather | solution.py:76
  275.7 9.1 %multiply_multiply_fusion = f32[1024,512]{1,0:T(8,128)S(1)} fusion(bf16[4096,1024]{1,0:T(8,128)(2,1)} %all-gather.5.cloned.1.call-done, bf16[4096,512]{1,0:T(8,128)(2,1)} %gather_fusion, pred[4096]{0:T(1024)(128)(4,1)S(1)} %compare_and_fusion, f32[1024]{0:T(1024)S(1)} %get-tuple-element.15, f32[512]{0:T(512)S(1)} %add_rsqrt_fusion), kind=kOutput, calls=%fused_computation.6 | convolution fusion | flops 4298113024 | bytes 14690304 | tf_op jit(solution)/shard_map/sv,sg->vg/dot_general | solution.py:32
  284.8 2.5 pad_maximum_fusion
  (19 shorter events, 0.2 us)
Async XLA Ops:
  6.5 20.0 %copy-start = (bf16[256,96]{0,1:T(8,128)(2,1)S(1)}, bf16[256,96]{0,1:T(8,128)(2,1)}, u32[]{:S(2)}) copy-start(bf16[256,96]{0,1:T(8,128)(2,1)} %param.10) | copy-start | bytes 147460
  6.5 113.9 %all-reduce.3.cloned.1.call-start = ((), (), s32[]{:S(2)}) async-start(), calls=%async_computation | async-start | bytes 1572864 | tf_op jit(solution)/shard_map/psum | solution.py:66
  28.0 99.5 %copy-start.1 = (s32[4096]{0:T(1024)S(1)}, s32[4096]{0:T(1024)}, u32[]{:S(2)}) copy-start(s32[4096]{0:T(1024)} %param.13) | copy-start | bytes 49156
  28.0 172.6 %all-gather.3.cloned.1.call-start = ((), (), s32[]{:S(2)}) async-start(), calls=%async_computation.1 | async-start | bytes 8912896 | tf_op jit(solution)/shard_map/all_gather | solution.py:76
  123.9 151.8 %all-gather.5.cloned.1.call-start = ((), (), s32[]{:S(2)}) async-start(), calls=%async_computation.2 | async-start | bytes 8912896 | tf_op jit(solution)/shard_map/all_gather | solution.py:76
Sparse Core Ops, SparseCore 0:
  28.1 92.2 all-reduce.2
  124.0 76.5 all-gather.2
  202.8 72.8 all-gather.4
where the time goes:
time: 296 us; the launch traced here: 294 us
  waiting for transfers between devices  112 us (38%)
  blocking collectives  78 us (26%)
  local copies, waits for them, and re-layouts  40.2 us (14%)
  matrix products  25.8 us (9%)
  other arithmetic  24.2 us (8%)
  between operations  13.3 us (4%)
    all_gather x2, waiting for transfers between devices, local(): lax.all_gather(part, 'samp', axis=0, tiled=True)  87.2 us
    psum x1, blocking collectives, local(): gram, loads = lax.psum((local_gram, jnp.stack(partials)), 'samp')  49.5 us
    psum x1, blocking collectives, finish(): lax.psum(jnp.sum(jnp.square(resid.astype(jnp.float32)), axis=0), 'samp')  28.5 us
    psum x1, waiting for transfers between devices, local(): gram, loads = lax.psum((local_gram, jnp.stack(partials)), 'samp')  25 us
    gather x1, local copies, waits for them, and re-layouts, fold(): rows = jnp.take(expression, expr_row, axis=0)  20.2 us
    dot_general x2, matrix products, fold(): jnp.einsum('sv,sg->vg', piece, rows, preferred_element_type=jnp.float32)  18.3 us
    gather x4, local copies, waits for them, and re-layouts, local(): jnp.take(dosage, block_index[block], axis=1)  12.8 us
    another operation x3, other arithmetic, local(): factor = jnp.linalg.cholesky(gram)  9.53 us
  transfers between devices with their start and end apart: 3, of which 3 were waited for; matrix products, arithmetic and copies ran while one was open for 18% of the time, Pallas kernels for 0%

commit v1 on v0

v1 whole, which is shorter than its diff:
```python
import functools
import math

import jax
import jax.numpy as jnp
from jax import lax
from jax.experimental import pallas as pl
from jax.experimental.pallas import tpu as pltpu
from jax.sharding import PartitionSpec as P

epsilon = 1e-06
MESH = pl.DeviceIdType.MESH
CHUNKS = 4


def exchange(n, p_ref, c_ref, expr_ref, row_ref, outp, outc, outm, norm_ref, ef, mf,
             send_sem, recv_sem, local_sem):
    depth = n // 4
    me = lax.axis_index("samp")
    z, y, core = me // 4, (me // 2) % 2, me % 2
    group = lax.axis_index("groups")
    width = p_ref.shape[0] // CHUNKS
    here = p_ref.shape[1]

    def index(zz, yy, cc):
        return (zz * 2 + yy) * 2 + cc

    def target(s):
        return (group, s)

    y_peer = index(z, 1 - y, core)
    core_peer = index(z, y, 1 - core)
    z_peers = [index(lax.rem(z + j, depth), y, core) for j in range(1, depth)]
    z_from = [index(lax.rem(z + depth - j, depth), y, core) for j in range(1, depth)]

    barrier = pltpu.get_barrier_semaphore()
    for peer in [y_peer, core_peer] + z_peers:
        pl.semaphore_signal(barrier, inc=1, device_id=target(peer), device_id_type=MESH)
    pl.semaphore_wait(barrier, depth + 1)

    pieces = CHUNKS + 1

    def stripe(owner):
        return pl.ds(pl.multiple_of(owner * here, here), here)

    def dst(piece, owner):
        if piece == 0:
            return outc.at[:, stripe(owner)]
        return outp.at[pl.ds((piece - 1) * width, width), stripe(owner)]

    def own(piece):
        if piece == 0:
            return c_ref
        return p_ref.at[pl.ds((piece - 1) * width, width), :]

    started = []

    def send(piece, owner, peer, src):
        k = len(started)
        copy = pltpu.make_async_remote_copy(
            src_ref=src, dst_ref=dst(piece, owner), send_sem=send_sem.at[k],
            recv_sem=recv_sem.at[piece, owner], device_id=target(peer), device_id_type=MESH)
        copy.start()
        started.append(copy)

    def arrive(piece, owner):
        pltpu.make_async_remote_copy(
            src_ref=own(piece), dst_ref=dst(piece, owner), send_sem=send_sem.at[0],
            recv_sem=recv_sem.at[piece, owner], device_id=target(y_peer),
            device_id_type=MESH).wait_recv()

    locals_ = []
    for piece in range(pieces):
        for peer in z_peers:
            send(piece, me, peer, own(piece))
        send(piece, me, y_peer, own(piece))
        send(piece, me, core_peer, own(piece))
        keep = pltpu.make_async_copy(own(piece), dst(piece, me), local_sem.at[piece])
        keep.start()
        locals_.append(keep)

    samples = expr_ref.shape[0]
    step = samples // 16
    norm_ref[...] = jnp.zeros_like(norm_ref)

    def widen(i, _):
        rows = pl.ds(pl.multiple_of(i * step, step), step)
        x = expr_ref[rows, :].astype(jnp.float32)
        ef[rows, :] = x
        norm_ref[...] += jnp.sum(x * x, axis=0, keepdims=True)
        return 0

    lax.fori_loop(0, 16, widen, 0)

    def match(low, high):
        def body(i, _):
            for u in range(16):
                j = i * 16 + u
                mf[pl.ds(u, 1), :] = ef[pl.ds(row_ref[j], 1), :]
            outm[pl.ds(pl.multiple_of(i * 16, 16), 16), :] = mf[...].astype(jnp.bfloat16)
            return 0
        lax.fori_loop(low, high, body, 0)

    spans = samples // 16
    cuts = [spans * p // pieces for p in range(pieces + 1)]
    for piece in range(pieces):
        arrive(piece, y_peer)
        send(piece, y_peer, core_peer, dst(piece, y_peer))
        for src in z_from:
            arrive(piece, src)
            send(piece, src, y_peer, dst(piece, src))
            send(piece, src, core_peer, dst(piece, src))
        if piece:
            late_y(piece - 1, z_from, arrive, send, core_peer, y, dst)
        match(cuts[piece], cuts[piece + 1])
    late_y(pieces - 1, z_from, arrive, send, core_peer, y, dst)
    for piece in range(pieces):
        for owner_z in range(depth):
            for owner_y in range(2):
                arrive(piece, index(owner_z, owner_y, 1 - core))
    for copy in started:
        copy.wait_send()
    for keep in locals_:
        keep.wait()


def late_y(piece, z_from, arrive, send, core_peer, y, dst):
    for src in z_from:
        other = src + 2 - 4 * y
        arrive(piece, other)
        send(piece, other, core_peer, dst(piece, other))


def finish(scale, p_ref, c_ref, k_ref, m_ref, norm_ref, out_ref, sums, sq):
    step, steps = pl.program_id(1), pl.num_programs(1)
    span = p_ref.shape[1]
    fitted = jnp.dot(k_ref[...], c_ref[...], preferred_element_type=jnp.float32)
    resid = (p_ref[...].astype(jnp.float32) - fitted).astype(jnp.bfloat16)
    wide = resid.astype(jnp.float32)
    rows = pl.ds(pl.multiple_of(step * span, span), span)
    part = jnp.dot(resid, m_ref[rows, :], preferred_element_type=jnp.float32)
    norm = jnp.sum(wide * wide, axis=1, keepdims=True)

    @pl.when(step == 0)
    def _():
        sums[...] = part
        sq[...] = norm

    @pl.when(step > 0)
    def _():
        sums[...] += part
        sq[...] += norm

    @pl.when(step == steps - 1)
    def _():
        out_ref[...] = (scale * sums[...] * lax.rsqrt(sq[...] + epsilon)
                        * lax.rsqrt(norm_ref[...] + epsilon))


def terms(x):
    first = lax.reduce_precision(x, 8, 7)
    rest = x - first
    second = lax.reduce_precision(rest, 8, 7)
    return [t.astype(jnp.bfloat16) for t in (first, second, rest - second)]


def local(n, dosage, covariates, expression, block_index, expr_row):
    blocks, block_width = block_index.shape
    covars = covariates.shape[1]
    here = covariates.shape[0]
    samples, genes = expression.shape
    variants = blocks * block_width
    scale = math.sqrt(samples - covars - 1)

    picked = jnp.take(dosage, block_index.reshape(-1), axis=1).T
    vmem = pl.BlockSpec(memory_space=pltpu.VMEM)
    anywhere = pl.BlockSpec(memory_space=pl.ANY)
    depth = n // 4
    pieces = CHUNKS + 1
    sends = pieces * (depth - 1 + 2 + 1 + 2 * (depth - 1) + depth - 1)
    everyone, covs, matched, panel_norm = pl.pallas_call(
        functools.partial(exchange, n),
        out_shape=(
            jax.ShapeDtypeStruct((variants, samples), jnp.bfloat16),
            jax.ShapeDtypeStruct((covars, samples), jnp.bfloat16),
            jax.ShapeDtypeStruct((samples, genes), jnp.bfloat16),
            jax.ShapeDtypeStruct((1, genes), jnp.float32),
        ),
        in_specs=[vmem, vmem, vmem, pl.BlockSpec(memory_space=pltpu.SMEM)],
        out_specs=(anywhere, anywhere, vmem, vmem),
        scratch_shapes=[
            pltpu.VMEM((samples, genes), jnp.float32),
            pltpu.VMEM((16, genes), jnp.float32),
            pltpu.SemaphoreType.DMA((sends,)),
            pltpu.SemaphoreType.DMA((pieces, n)),
            pltpu.SemaphoreType.DMA((pieces,)),
        ],
        compiler_params=pltpu.CompilerParams(
            collective_id=0, has_side_effects=True, vmem_limit_bytes=40 * 2**20),
    )(picked, covariates.T, expression, expr_row)

    gram = jnp.einsum("is,js->ij", covs, covs, preferred_element_type=jnp.float32)
    loads = jnp.einsum("is,vs->iv", covs, everyone, preferred_element_type=jnp.float32)
    factor = jnp.linalg.cholesky(gram)
    coeffs = jax.scipy.linalg.cho_solve((factor, True), loads)
    parts = jnp.concatenate(terms(coeffs.T), axis=1)
    covs3 = jnp.concatenate([covs] * 3, axis=0)
    tile, span = 512, min(1024, samples)
    return pl.pallas_call(
        functools.partial(finish, scale),
        out_shape=jax.ShapeDtypeStruct((variants, genes), jnp.float32),
        grid=(variants // tile, samples // span),
        in_specs=[
            pl.BlockSpec((tile, span), lambda i, j: (i, j)),
            pl.BlockSpec((3 * covars, span), lambda i, j: (0, j)),
            pl.BlockSpec((tile, 3 * covars), lambda i, j: (i, 0)),
            pl.BlockSpec((samples, genes), lambda i, j: (0, 0)),
            pl.BlockSpec((1, genes), lambda i, j: (0, 0)),
        ],
        out_specs=pl.BlockSpec((tile, genes), lambda i, j: (i, 0)),
        scratch_shapes=[
            pltpu.VMEM((tile, genes), jnp.float32),
            pltpu.VMEM((tile, 1), jnp.float32),
        ],
        compiler_params=pltpu.CompilerParams(vmem_limit_bytes=40 * 2**20),
    )(everyone, covs3, parts, matched, panel_norm)


def solution(mesh):
    placed = (
        P(("groups", "samp"), None),
        P(("groups", "samp"), None),
        P("groups", "samp"),
        P("groups", None),
        P("groups"),
    )
    return jax.shard_map(
        functools.partial(local, mesh.shape["samp"]),
        mesh=mesh, in_specs=placed, out_specs=P("groups", "samp"), check_vma=False
    )
```

time: 296 us -> 207 us (0.70)
  Pallas kernels: 0 us -> 148 us
  waiting for transfers between devices: 112 us -> 0 us
  blocking collectives: 78 us -> 0 us
  local copies, waits for them, and re-layouts: 40.2 us -> 23.4 us
  between operations: 13.3 us -> 0.18 us
  matrix products: 25.8 us -> 14 us
  other arithmetic: 24.2 us -> 20 us
    pallas_call x0 -> x2, Pallas kernels: none -> 148 us  [the longest x1 121 us: local(): pl.pallas_call(functools.partial(exchange, n), out_shape=(jax.ShapeDtypeS...]
    all_gather x2 -> x0, waiting for transfers between devices: 87.2 us -> none  [local(): lax.all_gather(part, 'samp', axis=0, tiled=True)]
    psum x2 -> x0, blocking collectives: 78 us -> none  [the longest x1 49.5 us: local(): gram, loads = lax.psum((local_gram, jnp.stack(partials)), 'samp')]
    psum x1 -> x0, waiting for transfers between devices: 25 us -> none  [local(): gram, loads = lax.psum((local_gram, jnp.stack(partials)), 'samp')]
    gather x5 -> x1, local copies, waits for them, and re-layouts: 33 us -> 9.36 us  [local(): picked = jnp.take(dosage, block_index.reshape(-1), axis=1).T]
    dot_general x7 -> x2, matrix products: 21.8 us -> 11.4 us  [the longest x1 11 us: local(): jnp.einsum('is,vs->iv', covs, everyone, preferred_element_type=jnp.float32)]
    unnamed x5 -> x12, local copies, waits for them, and re-layouts: 6.38 us -> 12.1 us
    reduce_sum x1 -> x0, other arithmetic: 3.15 us -> none  [local(): panel_norm = jnp.sum(jnp.square(expression.astype(jnp.float32)), axis=0)]
  transfers between devices with their start and end apart: 3 -> 0, of which waited for: 3 -> 0; matrix products, arithmetic and copies ran while one was open for 18% -> 0% of each run, Pallas kernels for 0% -> 0%
where the time goes in v1:
time: 207 us; the launch traced here: 206 us
  Pallas kernels  148 us (71%)
  local copies, waits for them, and re-layouts  23.4 us (11%)
  other arithmetic  20 us (10%)
  matrix products  14 us (7%)
    pallas_call x1, Pallas kernels, local(): pl.pallas_call(functools.partial(exchange, n), out_shape=(jax.ShapeDtypeS...  121 us
    pallas_call x1, Pallas kernels, local(): pl.pallas_call(functools.partial(finish, scale), out_shape=jax.ShapeDtype...  26.5 us
    unnamed x12, local copies, waits for them, and re-layouts  12.1 us
    dot_general x1, matrix products, local(): jnp.einsum('is,vs->iv', covs, everyone, preferred_element_type=jnp.float32)  11 us
    another operation x3, other arithmetic, local(): factor = jnp.linalg.cholesky(gram)  9.48 us
    gather x1, local copies, waits for them, and re-layouts, local(): picked = jnp.take(dosage, block_index.reshape(-1), axis=1).T  9.36 us
    another operation x2, other arithmetic, local(): coeffs = jax.scipy.linalg.cho_solve((factor, True), loads)  8 us

profile of v1, /device:TPU:9, one launch (start us, length us, event | category | flops | bytes accessed | tf_op | source)
XLA Modules:
  0.0 205.5 jit_solution(5743141851737229307)
XLA Ops:
  0.0 0.7 compare_and_fusion
  0.7 0.7 copy.16
  1.4 6.4 %copy.10 = bf16[256,8192]{0,1:T(8,128)(2,1)} copy(bf16[256,8192]{1,0:T(8,128)(2,1)} %param.5) | data formatting | bytes 8388608 | tf_op args[0]
  7.8 0.0 copy-start.3
  7.8 0.0 copy-start.4
  7.8 9.4 %gather_fusion = bf16[2048,256]{1,0:T(8,128)(2,1)S(1)} fusion(bf16[256,8192]{0,1:T(8,128)(2,1)} %copy.10, s32[2048]{0:T(1024)S(1)} %broadcast_clamp_fusion), kind=kCustom, calls=%fused_computation | custom fusion | bytes 2105344 | tf_op jit(solution)/shard_map/jit(_take)/gather | solution.py:175
  17.2 0.4 broadcast_select_fusion.p_ref
  17.6 0.0 copy-done.3
  17.7 0.0 copy-done.4
  17.7 0.0 copy-start.2
  17.7 2.2 %copy-done.2 = bf16[4096,512]{1,0:T(8,128)(2,1)S(1)} copy-done((bf16[4096,512]{1,0:T(8,128)(2,1)S(1)}, bf16[4096,512]{1,0:T(8,128)(2,1)}, u32[]{:S(2)}) %copy-start.2) | copy-done | bytes 4194328
  19.9 121.5 %shard_map.55 = (bf16[2048,4096]{1,0:T(8,128)(2,1)}, bf16[96,4096]{1,0:T(8,128)(2,1)S(1)}, bf16[4096,512]{1,0:T(8,128)(2,1)S(1)}, f32[1,512]{1,0:T(1,128)S(1)}) custom-call(bf16[2048,256]{1,0:T(8,128)(2,1)S(1)} %broadcast_select_fusion.p_ref, bf16[96,256]{1,0:T(8,128)(2,1)S(1)} %bitcast.30, bf16[4096,512]{1,0:T(8,128)(2,1)S(1)} %copy-done.2, s32[4096]{0:T(1024)S(1)} %copy-done.4), custom_call_target="tpu_custom_call" | custom-call | tf_op jit(solution)/shard_map/pallas_call | solution.py:181
  141.4 0.0 copy-start
  141.4 2.0 copy-done
  143.4 0.4 fusion.8
  143.7 0.1 copy.11
  143.8 8.8 %cholesky.16 = f32[96,96]{1,0:T(8,128)S(1)} custom-call(f32[96,96]{1,0:T(8,128)S(1)} %fusion.6), custom_call_target="Cholesky" | custom-call | tf_op jit(solution)/shard_map/jit(cholesky)/cholesky | solution.py:204
  152.7 0.7 compare_reduce_fusion
  153.3 0.6 fusion.1
  154.0 7.4 %custom-call.10 = f32[1,96,96]{1,2,0:T(8,128)S(1)} custom-call(f32[1,96,96]{2,1,0:T(8,128)S(1)} %fusion.1), custom_call_target="InvertDiagBlocksLowerTriangular" | custom-call | tf_op jit(solution)/shard_map/jit(_cho_solve)/triangular_solve | solution.py:205
  161.3 11.0 %fusion.9 = f32[96,2048]{1,0:T(8,128)S(1)} fusion(bf16[96,4096]{1,0:T(8,128)(2,1)S(1)} %get-tuple-element.10, bf16[2048,4096]{1,0:T(8,128)(2,1)} %get-tuple-element.9.p_ref), kind=kOutput, calls=%fused_computation.25 | convolution fusion | flops 1610612736 | bytes 18350080 | tf_op jit(solution)/shard_map/is,vs->iv/dot_general | solution.py:203
  172.4 0.9 fusion.4
  173.2 1.7 fusion.7
  175.0 0.3 copy.12
  175.3 1.5 copy.13
  176.8 0.0 copy-start.1
  176.8 0.2 reduce-precision_convert_fusion
  177.1 0.8 pad_maximum_fusion.1.k_ref
  177.9 0.3 pad_maximum_fusion.c_ref
  178.1 0.9 copy-done.1
  179.0 26.5 %shard_map.56 = f32[2048,512]{1,0:T(8,128)} custom-call(bf16[2048,4096]{1,0:T(8,128)(2,1)} %get-tuple-element.9.p_ref, bf16[288,4096]{1,0:T(8,128)(2,1)S(1)} %pad_maximum_fusion.c_ref, bf16[2048,288]{1,0:T(8,128)(2,1)S(1)} %pad_maximum_fusion.1.k_ref, bf16[4096,512]{1,0:T(8,128)(2,1)S(1)} %copy-done.1, f32[1,512]{1,0:T(1,128)S(1)} %get-tuple-element.12.norm_ref), custom_call_target="tpu_custom_call" | custom-call | tf_op jit(solution)/shard_map/pallas_call | solution.py:209
  (4 shorter events, 0.1 us)
Async XLA Ops:
  7.8 9.8 %copy-start.3 = (bf16[256,96]{0,1:T(8,128)(2,1)S(1)}, bf16[256,96]{0,1:T(8,128)(2,1)}, u32[]{:S(2)}) copy-start(bf16[256,96]{0,1:T(8,128)(2,1)} %param.6) | copy-start | bytes 147460
  7.8 9.8 %copy-start.4 = (s32[4096]{0:T(1024)S(1)}, s32[4096]{0:T(1024)}, u32[]{:S(2)}) copy-start(s32[4096]{0:T(1024)} %row_ref.1) | copy-start | bytes 49156
  17.7 2.2 %copy-start.2 = (bf16[4096,512]{1,0:T(8,128)(2,1)S(1)}, bf16[4096,512]{1,0:T(8,128)(2,1)}, u32[]{:S(2)}) copy-start(bf16[4096,512]{1,0:T(8,128)(2,1)} %expr_ref.1) | copy-start | bytes 12582916
  141.4 2.0 copy-start
  176.8 2.2 %copy-start.1 = (bf16[4096,512]{1,0:T(8,128)(2,1)S(1)}, bf16[4096,512]{1,0:T(8,128)(2,1)}, u32[]{:S(2)}) copy-start(bf16[4096,512]{1,0:T(8,128)(2,1)} %copy-done) | copy-start | bytes 12582916

commit v2 on v1

v2 whole, which is shorter than its diff:
```python
import functools
import math

import jax
import jax.numpy as jnp
from jax import lax
from jax.experimental import pallas as pl
from jax.experimental.pallas import tpu as pltpu
from jax.sharding import PartitionSpec as P

epsilon = 1e-06
MESH = pl.DeviceIdType.MESH
CHUNKS = 4
SPAN = 1024


def exchange(n, scale, p_ref, c_ref, expr_ref, row_ref, out_ref, panel, covs, matched,
             ef, mf, norm_ref, gram, right, lower, lower_scaled, sq, send_sem, recv_sem):
    depth = n // 4
    me = lax.axis_index("samp")
    z, y, core = me // 4, (me // 2) % 2, me % 2
    group = lax.axis_index("groups")
    width = p_ref.shape[0] // CHUNKS
    here = p_ref.shape[1]
    samples = expr_ref.shape[0]
    covars = c_ref.shape[0]

    def index(zz, yy, cc):
        return (zz * 2 + yy) * 2 + cc

    def target(s):
        return (group, s)

    y_peer = index(z, 1 - y, core)
    core_peer = index(z, y, 1 - core)
    z_peers = [index(lax.rem(z + j, depth), y, core) for j in range(1, depth)]
    z_from = [index(lax.rem(z + depth - j, depth), y, core) for j in range(1, depth)]

    barrier = pltpu.get_barrier_semaphore()
    for peer in [y_peer, core_peer] + z_peers:
        pl.semaphore_signal(barrier, inc=1, device_id=target(peer), device_id_type=MESH)
    pl.semaphore_wait(barrier, depth + 1)

    pieces = CHUNKS + 1

    def stripe(owner):
        return pl.ds(pl.multiple_of(owner * here, here), here)

    def dst(piece, owner):
        if piece == 0:
            return covs.at[:, stripe(owner)]
        return panel.at[pl.ds((piece - 1) * width, width), stripe(owner)]

    def own(piece):
        if piece == 0:
            return c_ref
        return p_ref.at[pl.ds((piece - 1) * width, width), :]

    started = []

    def send(piece, owner, peer, src):
        k = len(started)
        copy = pltpu.make_async_remote_copy(
            src_ref=src, dst_ref=dst(piece, owner), send_sem=send_sem.at[k],
            recv_sem=recv_sem.at[piece, owner], device_id=target(peer), device_id_type=MESH)
        copy.start()
        started.append(copy)

    def arrive(piece, owner):
        pltpu.make_async_remote_copy(
            src_ref=own(piece), dst_ref=dst(piece, owner), send_sem=send_sem.at[0],
            recv_sem=recv_sem.at[piece, owner], device_id=target(y_peer),
            device_id_type=MESH).wait_recv()

    for piece in range(pieces):
        for peer in z_peers:
            send(piece, me, peer, own(piece))
        send(piece, me, y_peer, own(piece))
        send(piece, me, core_peer, own(piece))
    covs[:, stripe(me)] = c_ref[...]
    panel[:, stripe(me)] = p_ref[...]

    step = samples // 16
    lanes = ef.shape[1]
    norm_ref[...] = jnp.zeros_like(norm_ref)

    def widen(part):
        genes = slice(part * lanes, (part + 1) * lanes)

        def body(i, _):
            rows = pl.ds(pl.multiple_of(i * step, step), step)
            x = expr_ref[rows, genes].astype(jnp.float32)
            ef[rows, :] = x
            norm_ref[:, genes] += jnp.sum(x * x, axis=0, keepdims=True)
            return 0

        lax.fori_loop(0, 16, body, 0)

    def match(part, low, high):
        genes = slice(part * lanes, (part + 1) * lanes)

        def body(i, _):
            for u in range(16):
                j = i * 16 + u
                mf[pl.ds(u, 1), :] = ef[pl.ds(row_ref[j], 1), :]
            rows = pl.ds(pl.multiple_of(i * 16, 16), 16)
            matched[rows, genes] = mf[...].astype(jnp.bfloat16)
            return 0

        lax.fori_loop(low, high, body, 0)

    def late(piece):
        for src in z_from:
            other = src + 2 - 4 * y
            arrive(piece, other)
            send(piece, other, core_peer, dst(piece, other))

    span = min(SPAN, samples)
    spans = samples // span
    columns = (((1,), (1,)), ((), ()))

    def cut(j):
        return pl.ds(pl.multiple_of(j * span, span), span)

    def eliminate():
        gram[...] = jnp.zeros_like(gram)

        def add(j, _):
            c = covs[:, cut(j)]
            gram[...] += lax.dot_general(c, c, columns, preferred_element_type=jnp.float32)
            return 0

        lax.fori_loop(0, spans, add, 0)
        row = lax.broadcasted_iota(jnp.int32, (covars, covars), 0)
        lane = lax.broadcasted_iota(jnp.int32, (covars, covars), 1)
        right[...] = (row == lane).astype(jnp.float32)
        first_lane = lax.broadcasted_iota(jnp.int32, (1, covars), 1)
        first_row = lax.broadcasted_iota(jnp.int32, (covars, 1), 0)

        def body(i, _):
            g_row, r_row = gram[pl.ds(i, 1), :], right[pl.ds(i, 1), :]
            pivot = jnp.sum(jnp.where(first_lane == i, g_row, 0.0), axis=1, keepdims=True)
            g = gram[...]
            column = jnp.sum(jnp.where(lane == i, g, 0.0), axis=1, keepdims=True)
            factor = jnp.where(first_row > i, column / pivot, 0.0)
            lower[pl.ds(i, 1), :] = r_row
            lower_scaled[pl.ds(i, 1), :] = r_row / pivot
            gram[...] = g - factor * g_row
            right[...] = right[...] - factor * r_row
            return 0

        lax.fori_loop(0, covars, body, 0)

    def scan(chunk):
        rows = pl.ds(chunk * width, width)

        def load(j, total):
            return total + lax.dot_general(
                panel[rows, cut(j)], covs[:, cut(j)], columns,
                preferred_element_type=jnp.float32)

        loads = lax.fori_loop(0, spans, load, jnp.zeros((width, covars), jnp.float32))
        solved = lax.dot_general(loads, lower[...], columns, precision=lax.Precision.HIGHEST,
                                 preferred_element_type=jnp.float32)
        coeffs = jnp.dot(solved, lower_scaled[...], precision=lax.Precision.HIGHEST,
                         preferred_element_type=jnp.float32)
        parts = jnp.concatenate(terms(coeffs), axis=1)
        sq[...] = jnp.zeros_like(sq)

        def product(j, _):
            c = covs[:, cut(j)]
            fitted = jnp.dot(parts, jnp.concatenate([c, c, c], axis=0),
                             preferred_element_type=jnp.float32)
            resid = (panel[rows, cut(j)].astype(jnp.float32) - fitted).astype(jnp.bfloat16)
            wide = resid.astype(jnp.float32)
            sq[...] += jnp.sum(wide * wide, axis=1, keepdims=True)
            part = jnp.dot(resid, matched[cut(j), :], preferred_element_type=jnp.float32)

            @pl.when(j == 0)
            def _():
                out_ref[rows, :] = part

            @pl.when(j > 0)
            def _():
                out_ref[rows, :] += part
            return 0

        lax.fori_loop(0, spans, product, 0)
        out_ref[rows, :] = (scale * out_ref[rows, :] * lax.rsqrt(sq[...] + epsilon)
                            * lax.rsqrt(norm_ref[...] + epsilon))

    def stage(piece):
        for owner_z in range(depth):
            for owner_y in range(2):
                arrive(piece, index(owner_z, owner_y, 1 - core))
        if piece == 0:
            eliminate()
        else:
            scan(piece - 1)

    groups16 = samples // 16
    halves = [groups16 * p // 3 for p in range(4)]
    rest = expr_ref.shape[1] // lanes - 1
    widen(0)
    for piece in range(pieces):
        arrive(piece, y_peer)
        send(piece, y_peer, core_peer, dst(piece, y_peer))
        for src in z_from:
            arrive(piece, src)
            send(piece, src, y_peer, dst(piece, src))
            send(piece, src, core_peer, dst(piece, src))
        if piece:
            late(piece - 1)
        if piece < 3:
            match(0, halves[piece], halves[piece + 1])
        if piece == 2:
            for part in range(1, rest + 1):
                widen(part)
                match(part, 0, groups16)
        if piece >= 2:
            stage(piece - 2)
    stage(pieces - 2)
    late(pieces - 1)
    stage(pieces - 1)
    for copy in started:
        copy.wait_send()


def terms(x):
    first = x.astype(jnp.bfloat16)
    rest = x - first.astype(jnp.float32)
    second = rest.astype(jnp.bfloat16)
    return [first, second, (rest - second.astype(jnp.float32)).astype(jnp.bfloat16)]


def local(n, dosage, covariates, expression, block_index, expr_row):
    blocks, block_width = block_index.shape
    covars = covariates.shape[1]
    samples, genes = expression.shape
    variants = blocks * block_width
    scale = math.sqrt(samples - covars - 1)

    picked = jnp.take(dosage, block_index.reshape(-1), axis=1).T
    vmem = pl.BlockSpec(memory_space=pltpu.VMEM)
    depth = n // 4
    pieces = CHUNKS + 1
    sends = pieces * (depth - 1 + 2 + 1 + 2 * (depth - 1) + depth - 1)
    lanes = genes if samples * genes * 4 <= 2**23 else 128
    square = pltpu.VMEM((covars, covars), jnp.float32)
    return pl.pallas_call(
        functools.partial(exchange, n, scale),
        out_shape=jax.ShapeDtypeStruct((variants, genes), jnp.float32),
        in_specs=[vmem, vmem, vmem, pl.BlockSpec(memory_space=pltpu.SMEM)],
        out_specs=vmem,
        scratch_shapes=[
            pltpu.VMEM((variants, samples), jnp.bfloat16),
            pltpu.VMEM((covars, samples), jnp.bfloat16),
            pltpu.VMEM((samples, genes), jnp.bfloat16),
            pltpu.VMEM((samples, lanes), jnp.float32),
            pltpu.VMEM((16, lanes), jnp.float32),
            pltpu.VMEM((1, genes), jnp.float32),
            square, square, square, square,
            pltpu.VMEM((variants // CHUNKS, 1), jnp.float32),
            pltpu.SemaphoreType.DMA((sends,)),
            pltpu.SemaphoreType.DMA((pieces, n)),
        ],
        compiler_params=pltpu.CompilerParams(
            collective_id=0, has_side_effects=True, vmem_limit_bytes=63 * 2**20),
    )(picked, covariates.T, expression, expr_row)


def solution(mesh):
    placed = (
        P(("groups", "samp"), None),
        P(("groups", "samp"), None),
        P("groups", "samp"),
        P("groups", None),
        P("groups"),
    )
    return jax.shard_map(
        functools.partial(local, mesh.shape["samp"]),
        mesh=mesh, in_specs=placed, out_specs=P("groups", "samp"), check_vma=False
    )
```

time: 207 us -> 166 us (0.80)
  other arithmetic: 20 us -> 1.95 us
  matrix products: 14 us -> 0 us
  Pallas kernels: 148 us -> 143 us
  local copies, waits for them, and re-layouts: 23.4 us -> 21.1 us
    another operation x5 -> x0, other arithmetic: 17.5 us -> none  [the longest x3 9.48 us: local(): factor = jnp.linalg.cholesky(gram)]
    dot_general x2 -> x0, matrix products: 11.4 us -> none  [the longest x1 11 us: local(): jnp.einsum('is,vs->iv', covs, everyone, preferred_element_type=jnp.float32)]
    pallas_call x2 -> x1, Pallas kernels: 148 us -> 143 us  [local(): pl.pallas_call(functools.partial(exchange, n, scale), out_shape=jax.Shape...]
    another operation x2 -> x0, matrix products: 2.6 us -> none  [local(): coeffs = jax.scipy.linalg.cho_solve((factor, True), loads)]
    unnamed x12 -> x3, local copies, waits for them, and re-layouts: 12.1 us -> 11.7 us
where the time goes in v2:
time: 166 us
  Pallas kernels  143 us (86%)
  local copies, waits for them, and re-layouts  21.1 us (13%)
  other arithmetic  1.95 us (1%)
    pallas_call x1, Pallas kernels, local(): pl.pallas_call(functools.partial(exchange, n, scale), out_shape=jax.Shape...  143 us
    unnamed x3, local copies, waits for them, and re-layouts  11.7 us
    gather x1, local copies, waits for them, and re-layouts, local(): picked = jnp.take(dosage, block_index.reshape(-1), axis=1).T  9.36 us

profile of v2, /device:TPU:9, one launch (start us, length us, event | category | flops | bytes accessed | tf_op | source)
XLA Modules:
  0.0 165.9 jit_solution(5065114397899473858)
XLA Ops:
  0.0 0.7 compare_and_fusion
  0.7 0.7 copy.8
  1.4 6.4 %copy.6 = bf16[256,8192]{0,1:T(8,128)(2,1)} copy(bf16[256,8192]{1,0:T(8,128)(2,1)} %param.5) | data formatting | bytes 8388608 | tf_op args[0]
  7.8 9.4 %gather_fusion = bf16[2048,256]{1,0:T(8,128)(2,1)S(1)} fusion(bf16[256,8192]{0,1:T(8,128)(2,1)} %copy.6, s32[2048]{0:T(1024)S(1)} %broadcast_clamp_fusion), kind=kCustom, calls=%fused_computation | custom fusion | bytes 2105344 | tf_op jit(solution)/shard_map/jit(_take)/gather | solution.py:243
  17.2 1.2 broadcast_select_fusion.p_ref
  18.4 142.8 %shard_map.55 = f32[2048,512]{1,0:T(8,128)} custom-call(bf16[2048,256]{1,0:T(8,128)(2,1)} %broadcast_select_fusion.p_ref, bf16[96,256]{1,0:T(8,128)(2,1)} %bitcast.11, bf16[4096,512]{1,0:T(8,128)(2,1)} %expr_ref.1, s32[4096]{0:T(1024)} %row_ref.1), custom_call_target="tpu_custom_call" | custom-call | tf_op jit(solution)/shard_map/pallas_call | solution.py:250
  161.2 4.6 %copy.13 = f32[2048,512]{1,0:T(8,128)} copy(f32[2048,512]{1,0:T(8,128)} %shard_map.55) | data formatting | bytes 8388608
  (2 shorter events, 0.0 us)
